TPU v7x, 512 devices: a whole 4x8x8 slice. The times are simulated.
512 devices in a mesh: chaos: 32 (over x, y), slab: 16 (over z, core).
Axes of the slice: x: 4, y: 8, z: 8, core: 2. Of those that a mesh axis runs over, the one named last changes fastest.
Arguments:
- displacement: float32 [288, 3, 12288], P('chaos', None, 'slab'), may hold values from -1.5 to 1.5
- load: float32 [288, 3, 12288], P('chaos', None, 'slab'), may hold values from -12 to 12
- mean_modulus: float32 [12288], P('slab'), may hold values from 0.5 to 2
- modes: float32 [10, 12288], P(None, 'slab'), may hold values from -0.6 to 0.6
- owner: int32 [288], replicated, may hold values from 0 to 287, each once
Outputs:
- solution: float32 [288, 3, 12288], P('chaos', None, 'slab')
- residual: float32 [288, 3, 12288], P('chaos', None, 'slab')
Inputs may be any that keep to these rules, and one draw needn't show every extreme that they name: `owner`: each value appears exactly once. Slot s lies on device s // 9 of the chaos axis; values of 286 or more mark empty slots.
All inputs are finite; a program needn't handle non-finite values.
Results may differ from a plain program's by a relative error of at most 0.0003.
Values sent between devices are 32-bit elements; how exact they have to be, the bound alone decides.
A program may use at most 128 MiB of HBM per device.

v0:
```python
import math

import jax
import jax.numpy as jnp
import numpy as np
from jax import lax
from jax.sharding import PartitionSpec as P

NX = 24
NY = 32
KL = 10
DEG = 3
SWEEPS = 4
ITERS = 2


bound_high = 50.0
bound_low = 2.5


def passed_along(value, axis, steps):
    count = lax.axis_size(axis)
    first, last = (max(0, -steps), min(count, count - steps))
    return lax.ppermute(value, axis, [(source, source + steps) for source in range(first, last)])


def extended_2(cells, sides, width):
    for axis, dim in sides:
        count = lax.axis_size(axis)
        ends = count - 1
        head = lax.slice_in_dim(cells, 0, width, axis=dim)
        tail = lax.slice_in_dim(cells, cells.shape[dim] - width, cells.shape[dim], axis=dim)
        cells = jnp.concatenate(
            [
                lax.ppermute(tail, axis, [(i, (i + 1) % count) for i in range(ends)]),
                cells,
                lax.ppermute(head, axis, [((i + 1) % count, i) for i in range(ends)]),
            ],
            axis=dim,
        )
    return cells


def multi_indices():
    listing = [[]]
    for variable in range(KL):
        extended_list = []
        for prefix in listing:
            for degree in range(DEG + 1 - sum(prefix)):
                extended_list.append(prefix + [degree])
        listing = extended_list
    return listing


def chaos_tables():
    listing = multi_indices()
    lookup = {tuple(multi_entry): number for number, multi_entry in enumerate(listing)}
    number_all = len(listing)
    up_index = np.full((number_all, KL), number_all, np.int32)
    up_weight = np.zeros((number_all, KL), np.float32)
    down_index = np.full((number_all, KL), number_all, np.int32)
    down_weight = np.zeros((number_all, KL), np.float32)
    for number, multi_entry in enumerate(listing):
        for variable in range(KL):
            raised = list(multi_entry)
            raised[variable] += 1
            if tuple(raised) in lookup:
                up_index[number, variable] = lookup[tuple(raised)]
                up_weight[number, variable] = math.sqrt(multi_entry[variable] + 1)
            if multi_entry[variable] > 0:
                lowered = list(multi_entry)
                lowered[variable] -= 1
                down_index[number, variable] = lookup[tuple(lowered)]
                down_weight[number, variable] = math.sqrt(multi_entry[variable])
    return (up_index, up_weight, down_index, down_weight)


def slot_neighbours(owner):
    up_index, up_weight, down_index, down_weight = chaos_tables()
    number_all = up_index.shape[0]
    live_slots = owner < number_all
    clipped = jnp.minimum(owner, number_all - 1)
    inverse = jnp.argsort(owner)

    def to_slots(index_table, weight_table):
        targets = jnp.asarray(index_table)[clipped]
        present = (targets < number_all) & live_slots[:, None]
        slots_of = inverse[jnp.minimum(targets, number_all - 1)]
        weights = jnp.where(present, jnp.asarray(weight_table)[clipped], 0.0)
        return (jnp.where(present, slots_of, 0), weights.astype(jnp.float32))

    return (to_slots(up_index, up_weight), to_slots(down_index, down_weight), live_slots)


def plane_masks(length):
    position = jnp.arange(length, dtype=jnp.int32)
    return (position // NY % NX, position % NY)


def forward_flat(values, step_size, keep):
    shifted = jnp.concatenate(
        [values[..., step_size:], jnp.zeros_like(values[..., :step_size])], axis=-1
    )
    return jnp.where(keep, shifted, 0.0) - values


def backward_flat(values, step_size, keep):
    shifted = jnp.concatenate(
        [jnp.zeros_like(values[..., :step_size]), values[..., :-step_size]], axis=-1
    )
    return values - jnp.where(keep, shifted, 0.0)


def stiffness_flat(fields, modulus):
    plane_size = NX * NY
    lowered = [field_one[..., :-plane_size] for field_one in fields]
    raised = [field_one[..., plane_size:] for field_one in fields]
    across_x, along_y = plane_masks(lowered[0].shape[-1])
    inner_x, inner_y = plane_masks(lowered[0].shape[-1] - plane_size)

    def slope_of(component, direction):
        if direction == 2:
            return raised[component] - lowered[component]
        if direction == 0:
            return forward_flat(lowered[component], NY, across_x != NX - 1)
        return forward_flat(lowered[component], 1, along_y != NY - 1)

    spread = slope_of(0, 0) + slope_of(1, 1) + slope_of(2, 2)
    results = []
    for component in range(3):
        summed = 0.0
        for direction in range(3):
            gradient = slope_of(component, direction)
            if direction == component:
                gradient = gradient + spread
            flux_term = modulus * gradient
            if direction == 2:
                summed = summed + (flux_term[..., plane_size:] - flux_term[..., :-plane_size])
            elif direction == 0:
                summed = summed + backward_flat(flux_term[..., plane_size:], NY, inner_x != 0)
            else:
                summed = summed + backward_flat(flux_term[..., plane_size:], 1, inner_y != 0)
        results.append(-summed)
    return results


def chebyshev(residual_in, apply_mean):
    center_value = 0.5 * (bound_high + bound_low)
    half_width = 0.5 * (bound_high - bound_low)
    ratio_value = center_value / half_width
    update = residual_in / center_value
    increment = update
    rho_prev = 1.0 / ratio_value
    for sweep_turn in range(SWEEPS):
        rho_next = 1.0 / (2.0 * ratio_value - rho_prev)
        increment = rho_next * rho_prev * increment + 2.0 * rho_next / half_width * (
            residual_in - apply_mean(update)
        )
        update = update + increment
        rho_prev = rho_next
    return update


def per_device(displacement, load, mean_modulus, modes, owner):
    plane_size = NX * NY
    slots_dev = displacement.shape[0]
    slots_all = owner.shape[0]
    (slot_up, weight_up), (slot_down, weight_down), live_slots = slot_neighbours(owner)
    own_start = lax.axis_index("chaos") * slots_dev
    live_own = lax.dynamic_slice_in_dim(live_slots, own_start, slots_dev, 0)
    keep_mask = live_own[:, None, None]
    solution = jnp.where(keep_mask, displacement, 0.0)
    target = jnp.where(keep_mask, load, 0.0)
    moduli = jnp.concatenate([mean_modulus[None], modes], axis=0)
    rim_below = passed_along(moduli, "slab", 1)
    moduli_ext = jnp.concatenate([rim_below, moduli], axis=1)
    mean_ext = moduli_ext[0]

    def operator_gathered(field_in):
        own_ids = own_start + jnp.arange(slots_dev, dtype=jnp.int32)
        up_own = lax.dynamic_slice_in_dim(slot_up, own_start, slots_dev, 0)
        down_own = lax.dynamic_slice_in_dim(slot_down, own_start, slots_dev, 0)
        up_weight_own = lax.dynamic_slice_in_dim(weight_up, own_start, slots_dev, 0)
        down_weight_own = lax.dynamic_slice_in_dim(weight_down, own_start, slots_dev, 0)
        columns = jnp.arange(slots_all, dtype=jnp.int32)
        identity_part = jnp.where(
            (own_ids[:, None] == columns[None, :]) & live_own[:, None], 1.0, 0.0
        )
        hits_up = jnp.where(
            up_own[:, :, None] == columns[None, None, :], up_weight_own[:, :, None], 0.0
        )
        hits_down = jnp.where(
            down_own[:, :, None] == columns[None, None, :], down_weight_own[:, :, None], 0.0
        )
        coupling = jnp.concatenate(
            [identity_part[None], jnp.transpose(hits_up + hits_down, (1, 0, 2))], axis=0
        )
        gathered = lax.all_gather(field_in, "chaos", axis=0, tiled=True)
        mixed_terms = jnp.einsum(
            "kij,jca->kcia", coupling, gathered, precision=lax.Precision.HIGHEST
        )
        extended = extended_2(mixed_terms, (("slab", 3),), plane_size)
        images = stiffness_flat(
            [extended[:, component] for component in range(3)], moduli_ext[:, None]
        )
        return jnp.stack([jnp.sum(image_one, axis=0) for image_one in images], axis=1)

    def apply_mean(field_in):
        extended = extended_2(field_in, (("slab", 2),), plane_size)
        return jnp.stack(
            stiffness_flat([extended[:, component] for component in range(3)], mean_ext), axis=1
        )

    residual = target
    for iteration in range(ITERS):
        image_now = operator_gathered(solution)
        residual = target - image_now
        solution = solution + chebyshev(residual, apply_mean)
    return (solution, residual)


def solution(mesh):
    in_specs = (P("chaos", None, "slab"), P("chaos", None, "slab"), P("slab"), P(None, "slab"), P())
    out_specs = (P("chaos", None, "slab"), P("chaos", None, "slab"))
    return jax.shard_map(
        per_device, mesh=mesh, in_specs=in_specs, out_specs=out_specs, check_vma=False
    )
```

profile of v0, /device:TPU:193, one launch (start us, length us, event | category | flops | bytes accessed | tf_op | source)
XLA Modules:
  0.0 349.6 jit_solution(7344398465879181725)
XLA Ops:
  8.0 1.6 broadcast_select_fusion
  10.4 2.0 gather_fusion
  12.4 1.1 gather_fusion.3
  13.7 3.8 %sort.17 = (s32[288]{0:T(512)}, s32[288]{0:T(512)S(1)}) sort(s32[288]{0:T(512)S(1)} %copy-done.7, s32[288]{0:T(512)S(1)} %iota.283), dimensions={0}, to_apply=%region_0.0 | sort | flops 2592 | bytes 4608 | tf_op jit(solution)/shard_map/jit(argsort)/sort | solution.py:83
  17.5 17.4 %gather_fusion.1 = s32[2880]{0:T(1024)S(1)} fusion(s32[288]{0:T(512)S(1)} %get-tuple-element.3, s32[3072]{0:T(1024)S(1)} %pad_clamp_fusion.1), kind=kCustom, calls=%fused_computation.1 | custom fusion | bytes 34560 | tf_op jit(solution)/shard_map/gather | solution.py:88
  35.2 17.4 %gather_fusion.4 = s32[2880]{0:T(1024)S(1)} fusion(s32[288]{0:T(512)S(1)} %get-tuple-element.3, s32[3072]{0:T(1024)S(1)} %pad_clamp_fusion), kind=kCustom, calls=%fused_computation.4 | custom fusion | bytes 34560 | tf_op jit(solution)/shard_map/gather | solution.py:88
  52.8 1.1 gather_fusion.2
  53.9 1.1 gather_fusion.5
  55.4 40.8 %all-gather.3.cloned.1.call-done = f32[288,3,768]{2,1,0:T(4,128)} async-done(((f32[9,3,768]{2,1,0:T(4,128)}), f32[288,3,768]{2,1,0:T(4,128)}) %all-gather.3.cloned.1.call-update) | async-done | bytes 2654224 | tf_op jit(solution)/shard_map/all_gather | solution.py:198
  96.2 4.7 %fusion.4 = f32[11,3,9,768]{3,0,2,1:T(8,128)S(1)} fusion(f32[288,3,768,1]{2,1,0,3:T(4,128)} %bitcast.160, f32[10,9,288]{2,0,1:T(8,128)S(1)} %select_add_fusion, f32[1,9,288]{2,0,1:T(1,128)S(1)} %and_select_fusion), kind=kOutput, calls=%fused_computation.12 | convolution fusion | flops 788328320 | bytes 3680640 | tf_op jit(solution)/shard_map/kij,jca->kcia/dot_general | solution.py:199
  101.6 8.7 %collective-permute-start.1 = (f32[11,3,9,768]{3,1,2,0:T(4,128)S(1)}, f32[11,3,9,768]{3,1,2,0:T(4,128)S(1)}, u32[]{:S(2)}, u32[]{:S(2)}) collective-permute-start(f32[11,3,9,768]{3,1,2,0:T(4,128)S(1)} %copy.23), channel_id=1, source_target_pairs={{0,1},{1,2},{2,3},{3,4},{4,5},{5,6},{6,7},{7,8},{8,9},{9,10},{10,1... | collective-permute-start | bytes 2737160 | tf_op jit(solution)/shard_map/ppermute | solution.py:35
  110.3 1.9 collective-permute-start.2
  112.3 5.0 %collective-permute-start = (f32[11,768]{1,0:T(8,128)S(1)}, f32[11,768]{1,0:T(8,128)S(1)}, u32[]{:S(2)}, u32[]{:S(2)}) collective-permute-start(f32[11,768]{1,0:T(8,128)S(1)} %pad_maximum_fusion.13), channel_id=1, source_target_pairs={{0,1},{1,2},{2,3},{3,4},{4,5},{5,6},{6,7},{7,8},{8,9},{9,10},{10,1... | collective-permute-start | bytes 101384 | tf_op jit(solution)/shard_map/ppermute | solution.py:24
  117.4 7.0 %collective-permute-done = f32[11,768]{1,0:T(8,128)S(1)} collective-permute-done((f32[11,768]{1,0:T(8,128)S(1)}, f32[11,768]{1,0:T(8,128)S(1)}, u32[]{:S(2)}, u32[]{:S(2)}) %collective-permute-start) | collective-permute-done | bytes 33824 | tf_op jit(solution)/shard_map/ppermute | solution.py:24
  124.6 4.8 %collective-permute-done.2 = f32[11,3,9,768]{3,1,2,0:T(4,128)S(1)} collective-permute-done((f32[11,3,9,768]{3,1,2,0:T(4,128)S(1)}, f32[11,3,9,768]{3,1,2,0:T(4,128)S(1)}, u32[]{:S(2)}, u32[]{:S(2)}) %collective-permute-start.2) | collective-permute-done | bytes 912416 | tf_op jit(solution)/shard_map/ppermute | solution.py:37
  132.0 1.4 add_multiply_fusion.4
  135.7 1.9 collective-permute-start.3
  137.7 2.4 collective-permute-start.4
  140.1 5.2 %collective-permute-done.4 = f32[9,3,768]{2,0,1:T(8,128)S(1)} collective-permute-done((f32[9,3,768]{2,0,1:T(8,128)S(1)}, f32[9,3,768]{2,0,1:T(8,128)S(1)}, u32[]{:S(2)}, u32[]{:S(2)}) %collective-permute-start.4) | collective-permute-done | bytes 82976 | tf_op jit(solution)/shard_map/ppermute | solution.py:37
  146.5 1.9 collective-permute-start.5
  148.4 2.4 collective-permute-start.6
  150.9 5.2 %collective-permute-done.6 = f32[9,3,768]{2,0,1:T(8,128)S(1)} collective-permute-done((f32[9,3,768]{2,0,1:T(8,128)S(1)}, f32[9,3,768]{2,0,1:T(8,128)S(1)}, u32[]{:S(2)}, u32[]{:S(2)}) %collective-permute-start.6) | collective-permute-done | bytes 82976 | tf_op jit(solution)/shard_map/ppermute | solution.py:37
  157.3 1.9 collective-permute-start.7
  159.2 2.4 collective-permute-start.8
  161.7 5.2 %collective-permute-done.8 = f32[9,3,768]{2,0,1:T(8,128)S(1)} collective-permute-done((f32[9,3,768]{2,0,1:T(8,128)S(1)}, f32[9,3,768]{2,0,1:T(8,128)S(1)}, u32[]{:S(2)}, u32[]{:S(2)}) %collective-permute-start.8) | collective-permute-done | bytes 82976 | tf_op jit(solution)/shard_map/ppermute | solution.py:37
  168.2 1.9 collective-permute-start.10
  170.2 5.1 %collective-permute-start.9 = (f32[9,3,768]{2,1,0:T(4,128)S(1)}, f32[9,3,768]{2,1,0:T(4,128)S(1)}, u32[]{:S(2)}, u32[]{:S(2)}) collective-permute-start(f32[9,3,768]{2,1,0:T(4,128)S(1)} %copy_add_fusion.3), channel_id=1, source_target_pairs={{0,1},{1,2},{2,3},{3,4},{4,5},{5,6},{6,7},{7,8},{8,9},{9,10},{10,1... | collective-permute-start | bytes 248840 | tf_op jit(solution)/shard_map/ppermute | solution.py:35
  175.5 1.2 collective-permute-done.9
  179.4 79.9 %all-gather.5.cloned.1.call-done = f32[288,3,768]{2,1,0:T(4,128)} async-done(((f32[9,3,768]{2,1,0:T(4,128)}), f32[288,3,768]{2,1,0:T(4,128)}) %all-gather.5.cloned.1.call-update) | async-done | bytes 2654224 | tf_op jit(solution)/shard_map/all_gather | solution.py:198
  259.3 4.7 %fusion.7 = f32[11,3,9,768]{3,0,2,1:T(8,128)S(1)} fusion(f32[288,3,768,1]{2,1,0,3:T(4,128)} %bitcast.161, f32[10,9,288]{2,0,1:T(8,128)S(1)} %select_add_fusion, f32[1,9,288]{2,0,1:T(1,128)S(1)} %and_select_fusion), kind=kOutput, calls=%fused_computation.13 | convolution fusion | flops 788328320 | bytes 3680640 | tf_op jit(solution)/shard_map/kij,jca->kcia/dot_general | solution.py:199
  264.7 8.7 %collective-permute-start.11 = (f32[11,3,9,768]{3,1,2,0:T(4,128)S(1)}, f32[11,3,9,768]{3,1,2,0:T(4,128)S(1)}, u32[]{:S(2)}, u32[]{:S(2)}) collective-permute-start(f32[11,3,9,768]{3,1,2,0:T(4,128)S(1)} %copy.34), channel_id=1, source_target_pairs={{0,1},{1,2},{2,3},{3,4},{4,5},{5,6},{6,7},{7,8},{8,9},{9,10},{10,1... | collective-permute-start | bytes 2737160 | tf_op jit(solution)/shard_map/ppermute | solution.py:35
  273.4 1.9 collective-permute-start.12
  275.3 11.6 %collective-permute-done.11 = f32[11,3,9,768]{3,1,2,0:T(4,128)S(1)} collective-permute-done((f32[11,3,9,768]{3,1,2,0:T(4,128)S(1)}, f32[11,3,9,768]{3,1,2,0:T(4,128)S(1)}, u32[]{:S(2)}, u32[]{:S(2)}) %collective-permute-start.11) | collective-permute-done | bytes 912416 | tf_op jit(solution)/shard_map/ppermute | solution.py:35
  287.1 5.4 %collective-permute-done.12 = f32[11,3,9,768]{3,1,2,0:T(4,128)S(1)} collective-permute-done((f32[11,3,9,768]{3,1,2,0:T(4,128)S(1)}, f32[11,3,9,768]{3,1,2,0:T(4,128)S(1)}, u32[]{:S(2)}, u32[]{:S(2)}) %collective-permute-start.12) | collective-permute-done | bytes 912416 | tf_op jit(solution)/shard_map/ppermute | solution.py:37
  295.1 1.4 add_multiply_fusion.1
  298.3 1.9 collective-permute-start.13
  300.2 2.4 collective-permute-start.14
  302.7 5.2 %collective-permute-done.14 = f32[9,3,768]{2,0,1:T(8,128)S(1)} collective-permute-done((f32[9,3,768]{2,0,1:T(8,128)S(1)}, f32[9,3,768]{2,0,1:T(8,128)S(1)}, u32[]{:S(2)}, u32[]{:S(2)}) %collective-permute-start.14) | collective-permute-done | bytes 82976 | tf_op jit(solution)/shard_map/ppermute | solution.py:37
  309.1 1.9 collective-permute-start.15
  311.0 2.4 collective-permute-start.16
  313.4 5.2 %collective-permute-done.16 = f32[9,3,768]{2,0,1:T(8,128)S(1)} collective-permute-done((f32[9,3,768]{2,0,1:T(8,128)S(1)}, f32[9,3,768]{2,0,1:T(8,128)S(1)}, u32[]{:S(2)}, u32[]{:S(2)}) %collective-permute-start.16) | collective-permute-done | bytes 82976 | tf_op jit(solution)/shard_map/ppermute | solution.py:37
  319.9 1.9 collective-permute-start.17
  321.8 2.4 collective-permute-start.18
  324.2 5.2 %collective-permute-done.18 = f32[9,3,768]{2,0,1:T(8,128)S(1)} collective-permute-done((f32[9,3,768]{2,0,1:T(8,128)S(1)}, f32[9,3,768]{2,0,1:T(8,128)S(1)}, u32[]{:S(2)}, u32[]{:S(2)}) %collective-permute-start.18) | collective-permute-done | bytes 82976 | tf_op jit(solution)/shard_map/ppermute | solution.py:37
  330.7 1.9 collective-permute-start.19
  332.6 2.4 collective-permute-start.20
  335.7 4.6 %collective-permute-done.20 = f32[9,3,768]{2,0,1:T(8,128)S(1)} collective-permute-done((f32[9,3,768]{2,0,1:T(8,128)S(1)}, f32[9,3,768]{2,0,1:T(8,128)S(1)}, u32[]{:S(2)}, u32[]{:S(2)}) %collective-permute-start.20) | collective-permute-done | bytes 82976 | tf_op jit(solution)/shard_map/ppermute | solution.py:37
  342.0 0.8 fusion.44
  (261 shorter events, 24.8 us)
Async XLA Ops:
  7.2 5.2 %copy-start.2 = (s32[286,10]{1,0:T(8,128)S(1)}, s32[286,10]{1,0:T(8,128)}, u32[]{:S(2)}) copy-start(s32[286,10]{1,0:T(8,128)} %constant.270.clone) | copy-start | bytes 34324
  7.2 89.0 %all-gather.3.cloned.1.call-start = ((), (), s32[]{:S(2)}) async-start(), calls=%async_computation | async-start | bytes 3649536 | tf_op jit(solution)/shard_map/all_gather | solution.py:198
  9.7 249.6 %all-gather.5.cloned.1.call-start = ((), (), s32[]{:S(2)}) async-start(), calls=%async_computation.1 | async-start | bytes 3649536 | tf_op jit(solution)/shard_map/all_gather | solution.py:198
  10.4 3.3 copy-start.7
  35.2 17.6 %copy-start.1 = (f32[286,10]{1,0:T(8,128)S(1)}, f32[286,10]{1,0:T(8,128)}, u32[]{:S(2)}) copy-start(f32[286,10]{1,0:T(8,128)} %constant.269.clone) | copy-start | bytes 34324
  52.7 1.2 copy-start
  100.9 11.3 %copy-start.8 = (f32[768]{0:T(1024)S(1)}, f32[768]{0:T(1024)}, u32[]{:S(2)}) copy-start(f32[768]{0:T(1024)} %param.11) | copy-start | bytes 9220
  100.9 11.3 %copy-start.6 = (f32[10,768]{1,0:T(8,128)S(1)}, f32[10,768]{1,0:T(8,128)}, u32[]{:S(2)}) copy-start(f32[10,768]{1,0:T(8,128)} %param.12) | copy-start | bytes 92164
  101.6 22.8 %collective-permute-start.1 = (f32[11,3,9,768]{3,1,2,0:T(4,128)S(1)}, f32[11,3,9,768]{3,1,2,0:T(4,128)S(1)}, u32[]{:S(2)}, u32[]{:S(2)}) collective-permute-start(f32[11,3,9,768]{3,1,2,0:T(4,128)S(1)} %copy.23), channel_id=1, source_target_pairs={{0,1},{1,2},{2,3},{3,4},{4,5},{5,6},{6,7},{7,8},{8,9},{9,10},{10,1... | collective-permute-start | bytes 2737160 | tf_op jit(solution)/shard_map/ppermute | solution.py:35
  110.3 19.1 %collective-permute-start.2 = (f32[11,3,9,768]{3,1,2,0:T(4,128)S(1)}, f32[11,3,9,768]{3,1,2,0:T(4,128)S(1)}, u32[]{:S(2)}, u32[]{:S(2)}) collective-permute-start(f32[11,3,9,768]{3,1,2,0:T(4,128)S(1)} %copy.23), channel_id=1, source_target_pairs={{1,0},{2,1},{3,2},{4,3},{5,4},{6,5},{7,6},{8,7},{9,8},{10,9},{11,1... | collective-permute-start | bytes 2737160 | tf_op jit(solution)/shard_map/ppermute | solution.py:37
  112.3 12.1 %collective-permute-start = (f32[11,768]{1,0:T(8,128)S(1)}, f32[11,768]{1,0:T(8,128)S(1)}, u32[]{:S(2)}, u32[]{:S(2)}) collective-permute-start(f32[11,768]{1,0:T(8,128)S(1)} %pad_maximum_fusion.13), channel_id=1, source_target_pairs={{0,1},{1,2},{2,3},{3,4},{4,5},{5,6},{6,7},{7,8},{8,9},{9,10},{10,1... | collective-permute-start | bytes 101384 | tf_op jit(solution)/shard_map/ppermute | solution.py:24
  134.7 0.9 copy-start.4
  135.7 4.4 %collective-permute-start.3 = (f32[9,3,768]{2,0,1:T(8,128)S(1)}, f32[9,3,768]{2,0,1:T(8,128)S(1)}, u32[]{:S(2)}, u32[]{:S(2)}) collective-permute-start(f32[9,3,768]{2,0,1:T(8,128)S(1)} %get-tuple-element.36), channel_id=1, source_target_pairs={{0,1},{1,2},{2,3},{3,4},{4,5},{5,6},{6,7},{7,8},{8,9},{9,10},{10,1... | collective-permute-start | bytes 248840 | tf_op jit(solution)/shard_map/ppermute | solution.py:35
  137.7 7.7 %collective-permute-start.4 = (f32[9,3,768]{2,0,1:T(8,128)S(1)}, f32[9,3,768]{2,0,1:T(8,128)S(1)}, u32[]{:S(2)}, u32[]{:S(2)}) collective-permute-start(f32[9,3,768]{2,0,1:T(8,128)S(1)} %get-tuple-element.36), channel_id=1, source_target_pairs={{1,0},{2,1},{3,2},{4,3},{5,4},{6,5},{7,6},{8,7},{9,8},{10,9},{11,1... | collective-permute-start | bytes 248840 | tf_op jit(solution)/shard_map/ppermute | solution.py:37
  146.5 4.3 %collective-permute-start.5 = (f32[9,3,768]{2,0,1:T(8,128)S(1)}, f32[9,3,768]{2,0,1:T(8,128)S(1)}, u32[]{:S(2)}, u32[]{:S(2)}) collective-permute-start(f32[9,3,768]{2,0,1:T(8,128)S(1)} %fusion.64), channel_id=1, source_target_pairs={{0,1},{1,2},{2,3},{3,4},{4,5},{5,6},{6,7},{7,8},{8,9},{9,10},{10,1... | collective-permute-start | bytes 248840 | tf_op jit(solution)/shard_map/ppermute | solution.py:35
  148.4 7.7 %collective-permute-start.6 = (f32[9,3,768]{2,0,1:T(8,128)S(1)}, f32[9,3,768]{2,0,1:T(8,128)S(1)}, u32[]{:S(2)}, u32[]{:S(2)}) collective-permute-start(f32[9,3,768]{2,0,1:T(8,128)S(1)} %fusion.64), channel_id=1, source_target_pairs={{1,0},{2,1},{3,2},{4,3},{5,4},{6,5},{7,6},{8,7},{9,8},{10,9},{11,1... | collective-permute-start | bytes 248840 | tf_op jit(solution)/shard_map/ppermute | solution.py:37
  157.3 4.3 %collective-permute-start.7 = (f32[9,3,768]{2,0,1:T(8,128)S(1)}, f32[9,3,768]{2,0,1:T(8,128)S(1)}, u32[]{:S(2)}, u32[]{:S(2)}) collective-permute-start(f32[9,3,768]{2,0,1:T(8,128)S(1)} %fusion.194), channel_id=1, source_target_pairs={{0,1},{1,2},{2,3},{3,4},{4,5},{5,6},{6,7},{7,8},{8,9},{9,10},{10,1... | collective-permute-start | bytes 248840 | tf_op jit(solution)/shard_map/ppermute | solution.py:35
  159.2 7.7 %collective-permute-start.8 = (f32[9,3,768]{2,0,1:T(8,128)S(1)}, f32[9,3,768]{2,0,1:T(8,128)S(1)}, u32[]{:S(2)}, u32[]{:S(2)}) collective-permute-start(f32[9,3,768]{2,0,1:T(8,128)S(1)} %fusion.194), channel_id=1, source_target_pairs={{1,0},{2,1},{3,2},{4,3},{5,4},{6,5},{7,6},{8,7},{9,8},{10,9},{11,1... | collective-permute-start | bytes 248840 | tf_op jit(solution)/shard_map/ppermute | solution.py:37
  168.2 7.3 %collective-permute-start.10 = (f32[9,3,768]{2,1,0:T(4,128)S(1)}, f32[9,3,768]{2,1,0:T(4,128)S(1)}, u32[]{:S(2)}, u32[]{:S(2)}) collective-permute-start(f32[9,3,768]{2,1,0:T(4,128)S(1)} %copy_add_fusion.3), channel_id=1, source_target_pairs={{1,0},{2,1},{3,2},{4,3},{5,4},{6,5},{7,6},{8,7},{9,8},{10,9},{11,1... | collective-permute-start | bytes 248840 | tf_op jit(solution)/shard_map/ppermute | solution.py:37
  170.2 6.6 %collective-permute-start.9 = (f32[9,3,768]{2,1,0:T(4,128)S(1)}, f32[9,3,768]{2,1,0:T(4,128)S(1)}, u32[]{:S(2)}, u32[]{:S(2)}) collective-permute-start(f32[9,3,768]{2,1,0:T(4,128)S(1)} %copy_add_fusion.3), channel_id=1, source_target_pairs={{0,1},{1,2},{2,3},{3,4},{4,5},{5,6},{6,7},{7,8},{8,9},{9,10},{10,1... | collective-permute-start | bytes 248840 | tf_op jit(solution)/shard_map/ppermute | solution.py:35
  177.7 0.9 copy-start.5
  264.7 22.3 %collective-permute-start.11 = (f32[11,3,9,768]{3,1,2,0:T(4,128)S(1)}, f32[11,3,9,768]{3,1,2,0:T(4,128)S(1)}, u32[]{:S(2)}, u32[]{:S(2)}) collective-permute-start(f32[11,3,9,768]{3,1,2,0:T(4,128)S(1)} %copy.34), channel_id=1, source_target_pairs={{0,1},{1,2},{2,3},{3,4},{4,5},{5,6},{6,7},{7,8},{8,9},{9,10},{10,1... | collective-permute-start | bytes 2737160 | tf_op jit(solution)/shard_map/ppermute | solution.py:35
  273.4 19.1 %collective-permute-start.12 = (f32[11,3,9,768]{3,1,2,0:T(4,128)S(1)}, f32[11,3,9,768]{3,1,2,0:T(4,128)S(1)}, u32[]{:S(2)}, u32[]{:S(2)}) collective-permute-start(f32[11,3,9,768]{3,1,2,0:T(4,128)S(1)} %copy.34), channel_id=1, source_target_pairs={{1,0},{2,1},{3,2},{4,3},{5,4},{6,5},{7,6},{8,7},{9,8},{10,9},{11,1... | collective-permute-start | bytes 2737160 | tf_op jit(solution)/shard_map/ppermute | solution.py:37
  298.3 4.3 %collective-permute-start.13 = (f32[9,3,768]{2,0,1:T(8,128)S(1)}, f32[9,3,768]{2,0,1:T(8,128)S(1)}, u32[]{:S(2)}, u32[]{:S(2)}) collective-permute-start(f32[9,3,768]{2,0,1:T(8,128)S(1)} %get-tuple-element.22), channel_id=1, source_target_pairs={{0,1},{1,2},{2,3},{3,4},{4,5},{5,6},{6,7},{7,8},{8,9},{9,10},{10,1... | collective-permute-start | bytes 248840 | tf_op jit(solution)/shard_map/ppermute | solution.py:35
  300.2 7.7 %collective-permute-start.14 = (f32[9,3,768]{2,0,1:T(8,128)S(1)}, f32[9,3,768]{2,0,1:T(8,128)S(1)}, u32[]{:S(2)}, u32[]{:S(2)}) collective-permute-start(f32[9,3,768]{2,0,1:T(8,128)S(1)} %get-tuple-element.22), channel_id=1, source_target_pairs={{1,0},{2,1},{3,2},{4,3},{5,4},{6,5},{7,6},{8,7},{9,8},{10,9},{11,1... | collective-permute-start | bytes 248840 | tf_op jit(solution)/shard_map/ppermute | solution.py:37
  309.1 4.3 %collective-permute-start.15 = (f32[9,3,768]{2,0,1:T(8,128)S(1)}, f32[9,3,768]{2,0,1:T(8,128)S(1)}, u32[]{:S(2)}, u32[]{:S(2)}) collective-permute-start(f32[9,3,768]{2,0,1:T(8,128)S(1)} %fusion.63), channel_id=1, source_target_pairs={{0,1},{1,2},{2,3},{3,4},{4,5},{5,6},{6,7},{7,8},{8,9},{9,10},{10,1... | collective-permute-start | bytes 248840 | tf_op jit(solution)/shard_map/ppermute | solution.py:35
  311.0 7.7 %collective-permute-start.16 = (f32[9,3,768]{2,0,1:T(8,128)S(1)}, f32[9,3,768]{2,0,1:T(8,128)S(1)}, u32[]{:S(2)}, u32[]{:S(2)}) collective-permute-start(f32[9,3,768]{2,0,1:T(8,128)S(1)} %fusion.63), channel_id=1, source_target_pairs={{1,0},{2,1},{3,2},{4,3},{5,4},{6,5},{7,6},{8,7},{9,8},{10,9},{11,1... | collective-permute-start | bytes 248840 | tf_op jit(solution)/shard_map/ppermute | solution.py:37
  319.9 4.3 %collective-permute-start.17 = (f32[9,3,768]{2,0,1:T(8,128)S(1)}, f32[9,3,768]{2,0,1:T(8,128)S(1)}, u32[]{:S(2)}, u32[]{:S(2)}) collective-permute-start(f32[9,3,768]{2,0,1:T(8,128)S(1)} %fusion.195), channel_id=1, source_target_pairs={{0,1},{1,2},{2,3},{3,4},{4,5},{5,6},{6,7},{7,8},{8,9},{9,10},{10,1... | collective-permute-start | bytes 248840 | tf_op jit(solution)/shard_map/ppermute | solution.py:35
  321.8 7.7 %collective-permute-start.18 = (f32[9,3,768]{2,0,1:T(8,128)S(1)}, f32[9,3,768]{2,0,1:T(8,128)S(1)}, u32[]{:S(2)}, u32[]{:S(2)}) collective-permute-start(f32[9,3,768]{2,0,1:T(8,128)S(1)} %fusion.195), channel_id=1, source_target_pairs={{1,0},{2,1},{3,2},{4,3},{5,4},{6,5},{7,6},{8,7},{9,8},{10,9},{11,1... | collective-permute-start | bytes 248840 | tf_op jit(solution)/shard_map/ppermute | solution.py:37
  330.7 5.0 %collective-permute-start.19 = (f32[9,3,768]{2,0,1:T(8,128)S(1)}, f32[9,3,768]{2,0,1:T(8,128)S(1)}, u32[]{:S(2)}, u32[]{:S(2)}) collective-permute-start(f32[9,3,768]{2,0,1:T(8,128)S(1)} %get-tuple-element.63), channel_id=1, source_target_pairs={{0,1},{1,2},{2,3},{3,4},{4,5},{5,6},{6,7},{7,8},{8,9},{9,10},{10,1... | collective-permute-start | bytes 248840 | tf_op jit(solution)/shard_map/ppermute | solution.py:35
  332.6 7.7 %collective-permute-start.20 = (f32[9,3,768]{2,0,1:T(8,128)S(1)}, f32[9,3,768]{2,0,1:T(8,128)S(1)}, u32[]{:S(2)}, u32[]{:S(2)}) collective-permute-start(f32[9,3,768]{2,0,1:T(8,128)S(1)} %get-tuple-element.63), channel_id=1, source_target_pairs={{1,0},{2,1},{3,2},{4,3},{5,4},{6,5},{7,6},{8,7},{9,8},{10,9},{11,1... | collective-permute-start | bytes 248840 | tf_op jit(solution)/shard_map/ppermute | solution.py:37
  341.1 0.9 copy-start.3
Sparse Core Ops, SparseCore 0:
  11.7 84.4 all-gather.2
  179.5 79.7 all-gather.4
where the time goes:
time: 351 us; the launch traced here: 350 us
  waiting for transfers between devices  187 us (53%)
  starting transfers between devices  63.7 us (18%)
  local copies, waits for them, and re-layouts  54.1 us (15%)
  other arithmetic  19.4 us (6%)
  between operations  16 us (5%)
  matrix products  9.4 us (3%)
    all_gather x2, waiting for transfers between devices, operator_gathered(): gathered = lax.all_gather(field_in, 'chaos', axis=0, tiled=True)  121 us
    ppermute x10, waiting for transfers between devices, extended_2(): lax.ppermute(head, axis, [((i + 1) % count, i) for i in range(ends)])  46.5 us
    ppermute x10, starting transfers between devices, extended_2(): lax.ppermute(tail, axis, [(i, (i + 1) % count) for i in range(ends)])  36 us
    gather x4, local copies, waits for them, and re-layouts, to_slots(): slots_of = inverse[jnp.minimum(targets, number_all - 1)]  35.1 us
    ppermute x10, starting transfers between devices, extended_2(): lax.ppermute(head, axis, [((i + 1) % count, i) for i in range(ends)])  22.6 us
    ppermute x10, waiting for transfers between devices, extended_2(): lax.ppermute(tail, axis, [(i, (i + 1) % count) for i in range(ends)])  12.9 us
    dot_general x2, matrix products, operator_gathered(): jnp.einsum('kij,jca->kcia', coupling, gathered, precision=lax.Precision.H...  9.4 us
    slice x60, local copies, waits for them, and re-layouts, forward_flat(): values[..., step_size:]  7.69 us
  transfers between devices with their start and end apart: 23, of which 15 were waited for; matrix products, arithmetic and copies ran while one was open for 13% of the time, Pallas kernels for 0%

commit v1 on v0

v1 whole, which is shorter than its diff:
```python
import functools
import heapq
import itertools
import math

import jax
import jax.numpy as jnp
import numpy as np
from jax import lax
from jax.experimental import pallas as pl
from jax.experimental.pallas import tpu as pltpu
from jax.sharding import PartitionSpec as P

NX, NY, KL, DEG, SWEEPS, ITERS = 24, 32, 10, 3, 4, 2
PX, PY = 4, 8
SLOTS_DEV = 9
ROW = 6
PER_SLOT = 3 * ROW
BLOCK = 168
GROUPS = 3
GSLOTS = SLOTS_DEV // GROUPS
GROWS = 56
THETA, DELTA = 26.25, 23.75
MESH = pl.DeviceIdType.MESH
DIRS = {"x+": (1, 0), "x-": (-1, 0), "y+": (0, 1), "y-": (0, -1)}
PIECES = {
    ("A", None): (0, 64),
    ("A", 0): (0, 32),
    ("A", 1): (32, 32),
    ("B", None): (64, 104),
    ("B", 0): (64, 56),
    ("B", 1): (120, 48),
}


def relative(ox, oy):
    return ((ox + PX // 2 - 1) % PX - (PX // 2 - 1), (oy + PY // 2 - 1) % PY - (PY // 2 - 1))


def gather_plan():
    count = itertools.count()
    halves = {}

    def allowed(way, part, owner, half):
        sends = []
        first, second = ("x", "y") if part == "A" else ("y", "x")
        at = {"x": owner[0], "y": owner[1]}
        far = {"x": PX // 2, "y": PY // 2}

        def chain(axis):
            reach, last = abs(at[axis]), far[axis] - 1
            if reach < last:
                sends.append((way, part, owner, None))
            elif reach == last:
                sends.append((way, part, owner, 0 if way[1] == "+" else 1))

        chain(way[0])
        if way[0] == first:
            ready = half is None
            if not ready:
                halves[part, owner] = halves.get((part, owner), 0) + 1
                ready = halves[part, owner] == 2
            if ready:
                sends.append((second + "+", part, owner, None))
                sends.append((second + "-", part, owner, None))
        return sends

    start = [(d, p, (0, 0), None) for p, d in (("A", "x+"), ("B", "y+"), ("A", "x-"), ("B", "y-"))]
    start += [(d, p, (0, 0), None) for p, d in (("A", "y+"), ("B", "x+"), ("A", "y-"), ("B", "x-"))]
    queues, busy, events, arrivals = {d: [] for d in DIRS}, dict.fromkeys(DIRS, False), [], []

    def begin(way, now):
        if queues[way] and not busy[way]:
            message = queues[way].pop(0)
            busy[way] = True
            took = PIECES[message[1], message[3]][1] / 91.0
            heapq.heappush(events, (now + took, next(count), "sent", message))
            heapq.heappush(events, (now + took + 2.0, next(count), "here", message))

    for message in start:
        queues[message[0]].append(message)
    for way in DIRS:
        begin(way, 0.0)
    while events:
        now, _, kind, message = heapq.heappop(events)
        way, part, owner, half = message
        if kind == "sent":
            busy[way] = False
        else:
            owner = relative(owner[0] - DIRS[way][0], owner[1] - DIRS[way][1])
            sends = allowed(way, part, owner, half)
            arrivals.append(((way, part, owner, half), sends))
            for send in sends:
                queues[send[0]].append(send)
        for each in DIRS:
            begin(each, now)
    return start, arrivals


def multi_indices():
    listing = [[]]
    for variable in range(KL):
        extended = []
        for prefix in listing:
            for degree in range(DEG + 1 - sum(prefix)):
                extended.append(prefix + [degree])
        listing = extended
    return listing


def chaos_tables(slots_all):
    listing = multi_indices()
    lookup = {tuple(entry): number for number, entry in enumerate(listing)}
    targets = np.full((2 * KL, slots_all), -1, np.int32)
    weights = np.zeros((2 * KL, slots_all), np.float32)
    for number, entry in enumerate(listing):
        for variable in range(KL):
            for side, step in ((0, 1), (1, -1)):
                other = list(entry)
                other[variable] += step
                if tuple(other) in lookup:
                    targets[side * KL + variable, number] = lookup[tuple(other)]
                    weights[side * KL + variable, number] = math.sqrt(
                        max(entry[variable], other[variable])
                    )
    return len(listing), targets, weights


def neighbour_tables(owner):
    slots_all = owner.shape[0]
    number_all, targets, weights = chaos_tables(slots_all)
    own = lax.dynamic_slice_in_dim(owner, lax.axis_index("chaos") * SLOTS_DEV, SLOTS_DEV, 0)
    numbers = jnp.arange(slots_all, dtype=jnp.int32)
    chosen = own[:, None, None] == numbers
    target = jnp.sum(jnp.where(chosen, jnp.asarray(targets), 0), axis=-1)
    weight = jnp.sum(jnp.where(chosen, jnp.asarray(weights), 0.0), axis=-1)
    rows = (numbers // SLOTS_DEV) * BLOCK + (numbers % SLOTS_DEV) * PER_SLOT
    row = jnp.sum(jnp.where(target[:, :, None] == owner, rows, 0), axis=-1)
    live = jnp.where(own < number_all, 1.0, 0.0)
    return row, jnp.concatenate([weight, live[:, None]], axis=1)


def kernel(
    rows_ref,
    weight_ref,
    disp_ref,
    load_ref,
    moduli_ref,
    sol_ref,
    res_ref,
    gathered_0,
    gathered_1,
    u_ref,
    f_ref,
    r_ref,
    z_ref,
    p_ref,
    t_ref,
    mod,
    mod_low,
    mod_x,
    mod_y,
    up_out,
    down_out,
    up_in,
    down_in,
    ag_send,
    ag_recv,
    up_send,
    up_recv,
    down_send,
    down_recv,
    mod_send,
    mod_recv,
):
    chaos = lax.axis_index("chaos")
    slab = lax.axis_index("slab")
    slabs = lax.axis_size("slab")
    cx, cy = chaos // PY, chaos % PY
    has_low, has_high = slab > 0, slab < slabs - 1

    def chaos_at(dx, dy):
        return lax.rem(cx + dx + PX, PX) * PY + lax.rem(cy + dy + PY, PY)

    lane = lax.broadcasted_iota(jnp.int32, (8, 128), 1)
    sub = lax.broadcasted_iota(jnp.int32, (8, 128), 0)
    inside = sub < ROW
    first_y = lane % NY == 0
    zero = jnp.zeros((8, 128), jnp.float32)

    def up_x(f):
        rolled = pltpu.roll(f, 128 - NY, 1)
        return jnp.where(lane < 128 - NY, rolled, pltpu.roll(rolled, 7, 0))

    def down_x(f):
        rolled = pltpu.roll(f, NY, 1)
        return jnp.where(lane < NY, pltpu.roll(rolled, 1, 0), rolled)

    def up_y(f):
        return pltpu.roll(f, 127, 1)

    def down_y(f):
        return jnp.where(first_y, 0.0, pltpu.roll(f, 1, 1))

    barrier = pltpu.get_barrier_semaphore()
    for dx, dy in DIRS.values():
        pl.semaphore_signal(
            barrier, inc=1, device_id=(chaos_at(dx, dy), slab), device_id_type=MESH
        )

    @pl.when(has_low)
    def _():
        pl.semaphore_signal(barrier, inc=1, device_id=(chaos, slab - 1), device_id_type=MESH)

    @pl.when(has_high)
    def _():
        pl.semaphore_signal(barrier, inc=1, device_id=(chaos, slab + 1), device_id_type=MESH)

    for ref in (u_ref, z_ref):
        ref[BLOCK - 8 : BLOCK, :] = zero

    def take(s, _):
        live = weight_ref[s, 2 * KL]
        for c in range(3):
            for k in range(ROW):
                at = pl.ds(s * PER_SLOT + c * ROW + k, 1)
                piece = disp_ref[s, c : c + 1, 128 * k : 128 * k + 128]
                u_ref[at, :] = jnp.where(live > 0.5, piece, 0.0)
                piece = load_ref[s, c : c + 1, 128 * k : 128 * k + 128]
                f_ref[at, :] = jnp.where(live > 0.5, piece, 0.0)
        return 0

    lax.fori_loop(0, SLOTS_DEV, take, 0)
    for v in range(KL + 1):
        mod[v] = zero
        for k in range(ROW):
            mod[v, k : k + 1, :] = moduli_ref[v : v + 1, 128 * k : 128 * k + 128]

    @pl.when(jnp.logical_not(has_low))
    def _():
        for v in range(KL + 1):
            mod_low[v] = zero

        def clear(i, _):
            up_in[i] = jnp.zeros((GROWS, 128), jnp.float32)
            return 0

        lax.fori_loop(0, ITERS * (SWEEPS + 1) * GROUPS, clear, 0)

    @pl.when(jnp.logical_not(has_high))
    def _():
        def clear(i, _):
            down_in[i] = jnp.zeros((GROWS, 128), jnp.float32)
            return 0

        lax.fori_loop(0, ITERS * (SWEEPS + 1) * GROUPS, clear, 0)

    neighbours = len(DIRS) + has_low.astype(jnp.int32) + has_high.astype(jnp.int32)
    pl.semaphore_wait(barrier, neighbours)

    mod_copy = pltpu.make_async_remote_copy(
        src_ref=mod,
        dst_ref=mod_low,
        send_sem=mod_send,
        recv_sem=mod_recv,
        device_id=(chaos, slab + 1),
        device_id_type=MESH,
    )

    @pl.when(has_high)
    def _():
        mod_copy.start()

    blocks = (gathered_0, gathered_1)
    start, arrivals = gather_plan()
    ids = {arrival: number for number, (arrival, _) in enumerate(arrivals)}

    def gather_copy(turn, way, part, owner, half):
        dx, dy = DIRS[way]
        number = ids[way, part, relative(owner[0] - dx, owner[1] - dy), half]
        first, size = PIECES[part, half]
        base = chaos_at(*owner) * BLOCK + first
        piece = blocks[turn].at[pl.ds(pl.multiple_of(base, 8), size)]
        return pltpu.make_async_remote_copy(
            src_ref=piece,
            dst_ref=piece,
            send_sem=ag_send.at[turn, number],
            recv_sem=ag_recv.at[turn, number],
            device_id=(chaos_at(dx, dy), slab),
            device_id_type=MESH,
        )

    def exchange(turn, k, g):
        i = (turn * (SWEEPS + 1) + k) * GROUPS + g
        up = pltpu.make_async_remote_copy(
            src_ref=up_out.at[i],
            dst_ref=up_in.at[i],
            send_sem=up_send.at[i],
            recv_sem=up_recv.at[i],
            device_id=(chaos, slab + 1),
            device_id_type=MESH,
        )
        down = pltpu.make_async_remote_copy(
            src_ref=down_out.at[i],
            dst_ref=down_in.at[i],
            send_sem=down_send.at[i],
            recv_sem=down_recv.at[i],
            device_id=(chaos, slab - 1),
            device_id_type=MESH,
        )
        return i, up, down

    def send(turn, k, g):
        _, up, down = exchange(turn, k, g)

        @pl.when(has_high)
        def _():
            up.start()

        @pl.when(has_low)
        def _():
            down.start()

    def receive(turn, k, g):
        _, up, down = exchange(turn, k, g)

        @pl.when(has_low)
        def _():
            up.wait_recv()

        @pl.when(has_high)
        def _():
            down.wait_recv()

    def sent(turn, k, g):
        _, up, down = exchange(turn, k, g)

        @pl.when(has_high)
        def _():
            up.wait_send()

        @pl.when(has_low)
        def _():
            down.wait_send()

    def own_part(i, g, j, at, x, y, z):
        px, py = [up_x(e) for e in x], [up_y(e) for e in y]
        spread = (px[0] - at[0]) + (py[1] - at[1]) - at[2]
        flux_x = [px[c] - at[c] for c in range(3)]
        flux_y = [py[c] - at[c] for c in range(3)]
        flux_x[0] = flux_x[0] + spread
        flux_y[1] = flux_y[1] + spread
        base = (g * GSLOTS + j) * PER_SLOT
        for c in range(3):
            total = (flux_x[c] - down_x(flux_x[c])) + (flux_y[c] - down_y(flux_y[c]))
            total = total - at[c] - z[c]
            if c == 2:
                total = total + spread - z[c]
            t_ref[pl.ds(base + c * ROW, ROW), :] = total[:ROW]
            low = at[c] if c < 2 else at[c] - spread
            inner = pl.ds(j * PER_SLOT + c * ROW, ROW)
            up_out[i, inner, :] = low[:ROW]
            down_out[i, inner, :] = z[c][:ROW]

    def minus_image(i, g, j):
        base = (g * GSLOTS + j) * PER_SLOT
        low = [up_in[i, pl.ds(j * PER_SLOT + c * ROW, 8), :] for c in range(3)]
        high = [down_in[i, pl.ds(j * PER_SLOT + c * ROW, 8), :] for c in range(3)]
        across = jnp.where(inside, high[2], 0.0)
        own = [t_ref[pl.ds(base + c * ROW, 8), :] for c in range(3)]
        return [
            own[0] + (across - down_x(across)) + high[0] + low[0],
            own[1] + (across - down_y(across)) + high[1] + low[1],
            own[2] + 2.0 * across + low[2],
        ]

    def slot_rows(g, j, c, size):
        return pl.ds((g * GSLOTS + j) * PER_SLOT + c * ROW, size)

    def mean_part(turn, k, g, j, z):
        i, _, _ = exchange(turn, k, g)
        own_part(
            i,
            g,
            j,
            [mod[0] * e for e in z],
            [mod_x[0] * e for e in z],
            [mod_y[0] * e for e in z],
            [mod_low[0] * e for e in z],
        )

    ratio = THETA / DELTA
    rho = 1.0 / ratio
    factors = []
    for _ in range(SWEEPS):
        rho_next = 1.0 / (2.0 * ratio - rho)
        factors.append((rho_next * rho, 2.0 * rho_next / DELTA))
        rho = rho_next

    def iteration(turn):
        gathered = blocks[turn]
        gathered[pl.ds(pl.multiple_of(chaos * BLOCK, 8), BLOCK), :] = u_ref[...]
        for message in start:
            gather_copy(turn, *message).start()

        if turn == 0:

            @pl.when(has_low)
            def _():
                mod_copy.wait_recv()

            for v in range(KL + 1):
                mod_x[v] = jnp.where(inside, down_x(mod[v]), 0.0)
                mod_y[v] = down_y(mod[v])

        for (way, part, owner, half), sends in arrivals:
            dx, dy = DIRS[way]
            first, size = PIECES[part, half]
            base = chaos_at(*owner) * BLOCK + first
            piece = blocks[turn].at[pl.ds(pl.multiple_of(base, 8), size)]
            number = ids[way, part, owner, half]
            pltpu.make_async_remote_copy(
                src_ref=piece,
                dst_ref=piece,
                send_sem=ag_send.at[turn, number],
                recv_sem=ag_recv.at[turn, number],
                device_id=(chaos_at(dx, dy), slab),
                device_id_type=MESH,
            ).wait_recv()
            for message in sends:
                gather_copy(turn, *message).start()

        def couple(g, _):
            i, _, _ = exchange(turn, 0, g)
            for j in range(GSLOTS):
                s = g * GSLOTS + j
                u = [u_ref[slot_rows(g, j, c, 8), :] for c in range(3)]
                at = [mod[0] * e for e in u]
                x = [mod_x[0] * e for e in u]
                y = [mod_y[0] * e for e in u]
                z = [mod_low[0] * e for e in u]
                for v in range(1, KL + 1):
                    up_row = rows_ref[s, v - 1]
                    down_row = rows_ref[s, KL + v - 1]
                    up_weight, down_weight = weight_ref[s, v - 1], weight_ref[s, KL + v - 1]
                    m, mx, my, mz = mod[v], mod_x[v], mod_y[v], mod_low[v]
                    for c in range(3):
                        e = up_weight * gathered[pl.ds(up_row + c * ROW, 8), :]
                        e = e + down_weight * gathered[pl.ds(down_row + c * ROW, 8), :]
                        at[c] = at[c] + m * e
                        x[c] = x[c] + mx * e
                        y[c] = y[c] + my * e
                        z[c] = z[c] + mz * e
                own_part(i, g, j, at, x, y, z)
            send(turn, 0, g)
            return 0

        lax.fori_loop(0, GROUPS, couple, 0)

        def first_update(g, _):
            receive(turn, 0, g)
            i, _, _ = exchange(turn, 0, g)
            for j in range(GSLOTS):
                image = minus_image(i, g, j)
                starts = []
                for c in range(3):
                    r = f_ref[slot_rows(g, j, c, 8), :] + image[c]
                    z = r * (1.0 / THETA)
                    rows = slot_rows(g, j, c, ROW)
                    r_ref[rows, :] = r[:ROW]
                    z_ref[rows, :] = z[:ROW]
                    p_ref[rows, :] = z[:ROW]
                    starts.append(jnp.where(inside, z, 0.0))
                mean_part(turn, 1, g, j, starts)
            send(turn, 1, g)
            return 0

        lax.fori_loop(0, GROUPS, first_update, 0)

        for k in range(1, SWEEPS + 1):
            keep, gain = factors[k - 1]

            def sweep(g, _, k=k, keep=keep, gain=gain):
                receive(turn, k, g)
                i, _, _ = exchange(turn, k, g)
                for j in range(GSLOTS):
                    image = minus_image(i, g, j)
                    updated = []
                    for c in range(3):
                        whole, rows = slot_rows(g, j, c, 8), slot_rows(g, j, c, ROW)
                        p = keep * p_ref[whole, :] + gain * (r_ref[whole, :] + image[c])
                        z = z_ref[whole, :] + p
                        if k < SWEEPS:
                            p_ref[rows, :] = p[:ROW]
                            z_ref[rows, :] = z[:ROW]
                            updated.append(jnp.where(inside, z, 0.0))
                        else:
                            u_ref[rows, :] = (u_ref[whole, :] + z)[:ROW]
                    if k < SWEEPS:
                        mean_part(turn, k + 1, g, j, updated)
                if k < SWEEPS:
                    send(turn, k + 1, g)
                return 0

            lax.fori_loop(0, GROUPS, sweep, 0)

    for turn in range(ITERS):
        iteration(turn)

    def give(s, _):
        for c in range(3):
            for k in range(ROW):
                at = pl.ds(s * PER_SLOT + c * ROW + k, 1)
                sol_ref[s, c : c + 1, 128 * k : 128 * k + 128] = u_ref[at, :]
                res_ref[s, c : c + 1, 128 * k : 128 * k + 128] = r_ref[at, :]
        return 0

    lax.fori_loop(0, SLOTS_DEV, give, 0)

    @pl.when(has_high)
    def _():
        mod_copy.wait_send()

    for turn in range(ITERS):
        for message in start:
            gather_copy(turn, *message).wait_send()
        for _, sends in arrivals:
            for message in sends:
                gather_copy(turn, *message).wait_send()
        for k in range(SWEEPS + 1):
            for g in range(GROUPS):
                sent(turn, k, g)


def per_device(displacement, load, mean_modulus, modes, owner):
    rows, weights = neighbour_tables(owner)
    moduli = jnp.concatenate([mean_modulus[None], modes], axis=0)
    _, arrivals = gather_plan()
    messages = len(arrivals)
    exchanges = ITERS * (SWEEPS + 1) * GROUPS
    field = pltpu.VMEM((BLOCK, 128), jnp.float32)
    moduli_field = pltpu.VMEM((KL + 1, 8, 128), jnp.float32)
    planes = pltpu.VMEM((exchanges, GROWS, 128), jnp.float32)
    out = jax.ShapeDtypeStruct(displacement.shape, jnp.float32)
    smem, vmem = pl.BlockSpec(memory_space=pltpu.SMEM), pl.BlockSpec(memory_space=pltpu.VMEM)
    dma = pltpu.SemaphoreType.DMA
    return pl.pallas_call(
        kernel,
        out_shape=(out, out),
        in_specs=[smem, smem, vmem, vmem, vmem],
        out_specs=(vmem, vmem),
        scratch_shapes=[
            pltpu.VMEM((PX * PY * BLOCK, 128), jnp.float32),
            pltpu.VMEM((PX * PY * BLOCK, 128), jnp.float32),
            field,
            field,
            field,
            field,
            field,
            field,
            moduli_field,
            moduli_field,
            moduli_field,
            moduli_field,
            planes,
            planes,
            planes,
            planes,
            dma((ITERS, messages)),
            dma((ITERS, messages)),
            dma((exchanges,)),
            dma((exchanges,)),
            dma((exchanges,)),
            dma((exchanges,)),
            dma,
            dma,
        ],
        compiler_params=pltpu.CompilerParams(collective_id=0, has_side_effects=True),
        name="galerkin",
    )(rows, weights, displacement, load, moduli)


def solution(mesh):
    in_specs = (P("chaos", None, "slab"), P("chaos", None, "slab"), P("slab"), P(None, "slab"), P())
    out_specs = (P("chaos", None, "slab"), P("chaos", None, "slab"))
    return jax.shard_map(
        per_device, mesh=mesh, in_specs=in_specs, out_specs=out_specs, check_vma=False
    )
```

time: 351 us -> 104 us (0.30)
  waiting for transfers between devices: 187 us -> 0 us
  Pallas kernels: 0 us -> 95.9 us
  starting transfers between devices: 63.7 us -> 0 us
  local copies, waits for them, and re-layouts: 54.1 us -> 3.48 us
  other arithmetic: 19.4 us -> 3.44 us
  between operations: 16 us -> 0.68 us
  matrix products: 9.4 us -> 0 us
    all_gather x2 -> x0, waiting for transfers between devices: 121 us -> none  [operator_gathered(): gathered = lax.all_gather(field_in, 'chaos', axis=0, tiled=True)]
    pallas_call x0 -> x1, Pallas kernels: none -> 95.9 us  [per_device(): pl.pallas_call(kernel, out_shape=(out, out), in_specs=[smem, smem, vmem,...]
    ppermute x21 -> x0, waiting for transfers between devices: 66.4 us -> none  [the longest x10 46.5 us: extended_2(): lax.ppermute(head, axis, [((i + 1) % count, i) for i in range(ends)])]
    ppermute x21 -> x0, starting transfers between devices: 63.6 us -> none  [the longest x10 36 us: extended_2(): lax.ppermute(tail, axis, [(i, (i + 1) % count) for i in range(ends)])]
    gather x8 -> x0, local copies, waits for them, and re-layouts: 40.3 us -> none  [the longest x4 35.1 us: to_slots(): slots_of = inverse[jnp.minimum(targets, number_all - 1)]]
    dot_general x2 -> x0, matrix products: 9.4 us -> none  [operator_gathered(): jnp.einsum('kij,jca->kcia', coupling, gathered, precision=lax.Precision.H...]
    slice x121 -> x0, local copies, waits for them, and re-layouts: 8.33 us -> none  [the longest x60 7.69 us: forward_flat(): values[..., step_size:]]
    mul x22 -> x0, other arithmetic: 5.18 us -> none  [the longest x20 5 us: stiffness_flat(): flux_term = modulus * gradient]
  transfers between devices with their start and end apart: 23 -> 0, of which waited for: 15 -> 0; matrix products, arithmetic and copies ran while one was open for 13% -> 0% of each run, Pallas kernels for 0% -> 0%
where the time goes in v1:
time: 104 us; the launch traced here: 103 us
  Pallas kernels  95.9 us (92%)
  local copies, waits for them, and re-layouts  3.48 us (3%)
  other arithmetic  3.44 us (3%)
    pallas_call x1, Pallas kernels, per_device(): pl.pallas_call(kernel, out_shape=(out, out), in_specs=[smem, smem, vmem,...  95.9 us
    unnamed x12, local copies, waits for them, and re-layouts  2.69 us

profile of v1, /device:TPU:193, one launch (start us, length us, event | category | flops | bytes accessed | tf_op | source)
XLA Modules:
  0.0 103.5 jit_solution(4670303509836682833)
XLA Ops:
  0.6 0.0 copy-start.3
  0.6 0.8 fusion.10
  1.4 0.7 broadcast_in_dim.63
  2.1 0.1 iota_compare_fusion
  2.2 0.1 copy.10
  2.3 0.0 copy-done.3
  2.3 0.0 copy-start.2
  2.3 0.1 select_reduce_fusion
  2.4 0.0 copy-start.1
  2.4 0.7 pad_maximum_fusion.1.weight_ref
  3.1 0.0 copy-done.2
  3.1 0.0 copy-start.4
  3.1 0.2 select_reduce_fusion.2
  3.3 0.4 copy-done.4
  3.8 0.9 select_reduce_fusion.1.rows_ref
  4.7 0.0 copy-done.1
  4.7 0.6 pad_maximum_fusion.moduli_ref
  5.3 95.9 %galerkin.1 = (f32[9,3,768]{2,1,0:T(4,128)}, f32[9,3,768]{2,1,0:T(4,128)}) custom-call(s32[9,20]{1,0:T(8,128)} %select_reduce_fusion.1.rows_ref, f32[9,21]{1,0:T(8,128)} %pad_maximum_fusion.1.weight_ref, f32[9,3,768]{2,1,0:T(4,128)} %disp_ref.1, f32[9,3,768]{2,1,0:T(4,128)} %load_ref.1, f32[11,768]{1,0:T(8,128)} %pad_maximum_fusion.moduli_ref), custom_call_target="tpu_custom_call" | custom-call | tf_op jit(solution)/shard_map/galerkin/pallas_call | solution.py:547
  101.2 0.0 copy-start
  101.2 1.6 %copy.13 = f32[9,3,768]{2,1,0:T(4,128)} copy(f32[9,3,768]{2,1,0:T(4,128)} %get-tuple-element.6) | data formatting | bytes 165888
  102.8 0.0 copy-done
  102.8 0.6 copy.14
  (1 shorter events, 0.0 us)
Async XLA Ops:
  0.6 1.7 %copy-start.3 = (f32[20,288]{1,0:T(8,128)S(1)}, f32[20,288]{1,0:T(8,128)}, u32[]{:S(2)}) copy-start(f32[20,288]{1,0:T(8,128)} %constant.44.clone) | copy-start | bytes 69124
  2.3 0.8 copy-start.2
  2.4 2.3 %copy-start.1 = (f32[10,768]{1,0:T(8,128)S(1)}, f32[10,768]{1,0:T(8,128)}, u32[]{:S(2)}) copy-start(f32[10,768]{1,0:T(8,128)} %param.10) | copy-start | bytes 92164
  3.1 0.7 copy-start.4
  101.2 1.6 %copy-start = (f32[9,3,768]{2,1,0:T(4,128)S(1)}, f32[9,3,768]{2,1,0:T(4,128)}, u32[]{:S(2)}) copy-start(f32[9,3,768]{2,1,0:T(4,128)} %get-tuple-element.7) | copy-start | bytes 248836

commit v2 on v1

--- a/solution.py
+++ b/solution.py
@@ -23,78 +23,104 @@
 THETA, DELTA = 26.25, 23.75
 MESH = pl.DeviceIdType.MESH
 DIRS = {"x+": (1, 0), "x-": (-1, 0), "y+": (0, 1), "y-": (0, -1)}
-PIECES = {
-    ("A", None): (0, 64),
-    ("A", 0): (0, 32),
-    ("A", 1): (32, 32),
-    ("B", None): (64, 104),
-    ("B", 0): (64, 56),
-    ("B", 1): (120, 48),
-}
+CHUNKS = (("x", 0, 64, 32), ("y", 64, 104, 56))
+MODES = {("x", 0): "leap", ("y", 0): "leap", ("x", 1): "chain", ("y", 1): "chain"}
+LATENCY, HOP, RATE, AHEAD = 2.8, 0.8, 88.0, 1.2
+
+
+def piece_rows(chunk, half):
+    _, first, size, upper = CHUNKS[chunk]
+    return {None: (first, size), 0: (first, upper), 1: (first + upper, size - upper)}[half]
 
 
 def relative(ox, oy):
     return ((ox + PX // 2 - 1) % PX - (PX // 2 - 1), (oy + PY // 2 - 1) % PY - (PY // 2 - 1))
+
+
+def onward(axis, stage, reach):
+    far = (PX if axis == "x" else PY) // 2
+    if MODES[axis, stage] == "chain":
+        return [(1, reach == far - 1)] if reach < far else []
+    if far == 2:
+        return [(1, False), (2, True)] if reach == 0 else []
+    return {0: [(1, False), (2, False)], 2: [(1, False), (2, True)]}.get(reach, [])
+
+
+def depth(axis, stage, reach):
+    return max((1 + depth(axis, stage, reach + hops) for hops, _ in onward(axis, stage, reach)), default=0)
 
 
 def gather_plan():
     count = itertools.count()
     halves = {}
 
-    def allowed(way, part, owner, half):
-        sends = []
-        first, second = ("x", "y") if part == "A" else ("y", "x")
-        at = {"x": owner[0], "y": owner[1]}
-        far = {"x": PX // 2, "y": PY // 2}
-
-        def chain(axis):
-            reach, last = abs(at[axis]), far[axis] - 1
-            if reach < last:
-                sends.append((way, part, owner, None))
-            elif reach == last:
-                sends.append((way, part, owner, 0 if way[1] == "+" else 1))
-
-        chain(way[0])
-        if way[0] == first:
-            ready = half is None
-            if not ready:
-                halves[part, owner] = halves.get((part, owner), 0) + 1
-                ready = halves[part, owner] == 2
-            if ready:
-                sends.append((second + "+", part, owner, None))
-                sends.append((second + "-", part, owner, None))
+    def carried(way, chunk, owner, stage):
+        reach = abs(owner["xy".index(way[0])])
+        return [
+            (way, hops, chunk, owner, (0 if way[1] == "+" else 1) if half else None)
+            for hops, half in onward(way[0], stage, reach)
+        ]
+
+    def allowed(way, chunk, owner, half):
+        first = CHUNKS[chunk][0]
+        if way[0] != first:
+            return carried(way, chunk, owner, 1)
+        sends = carried(way, chunk, owner, 0) if half is None else []
+        if half is not None:
+            halves[chunk, owner] = halves.get((chunk, owner), 0) + 1
+        if half is None or halves[chunk, owner] == 2:
+            second = "y" if first == "x" else "x"
+            for sign in "+-":
+                sends += carried(second + sign, chunk, owner, 1)
         return sends
 
-    start = [(d, p, (0, 0), None) for p, d in (("A", "x+"), ("B", "y+"), ("A", "x-"), ("B", "y-"))]
-    start += [(d, p, (0, 0), None) for p, d in (("A", "y+"), ("B", "x+"), ("A", "y-"), ("B", "x-"))]
-    queues, busy, events, arrivals = {d: [] for d in DIRS}, dict.fromkeys(DIRS, False), [], []
+    def urgency(message):
+        way, hops, chunk, owner, _ = message
+        axis, first = way[0], CHUNKS[chunk][0]
+        reach = abs(owner["xy".index(axis)]) + hops
+        if axis != first:
+            return -depth(axis, 1, reach)
+        return -depth(axis, 0, reach) - depth("y" if axis == "x" else "x", 1, 0)
+
+    queues, busy = {d: [] for d in DIRS}, dict.fromkeys(DIRS, False)
+    events, steps = [], []
+
+    def put(message, now):
+        heapq.heappush(queues[message[0]], (urgency(message), next(count), message, now))
 
     def begin(way, now):
         if queues[way] and not busy[way]:
-            message = queues[way].pop(0)
+            _, _, message, since = heapq.heappop(queues[way])
             busy[way] = True
-            took = PIECES[message[1], message[3]][1] / 91.0
+            steps.append((max(since, now - AHEAD), next(count), "send", message))
+            hops = message[1]
+            took = hops * piece_rows(message[2], message[4])[1] / RATE
             heapq.heappush(events, (now + took, next(count), "sent", message))
-            heapq.heappush(events, (now + took + 2.0, next(count), "here", message))
-
-    for message in start:
-        queues[message[0]].append(message)
+            here = now + took + LATENCY + HOP * (hops - 1)
+            heapq.heappush(events, (here, next(count), "here", message))
+
+    for stage in (0, 1):
+        for sign in "+-":
+            for chunk, (first, *_) in enumerate(CHUNKS):
+                axis = first if stage == 0 else "y" if first == "x" else "x"
+                for message in carried(axis + sign, chunk, (0, 0), stage):
+                    put(message, 0.0)
     for way in DIRS:
         begin(way, 0.0)
     while events:
         now, _, kind, message = heapq.heappop(events)
-        way, part, owner, half = message
+        way, hops, chunk, owner, half = message
         if kind == "sent":
             busy[way] = False
         else:
-            owner = relative(owner[0] - DIRS[way][0], owner[1] - DIRS[way][1])
-            sends = allowed(way, part, owner, half)
-            arrivals.append(((way, part, owner, half), sends))
-            for send in sends:
-                queues[send[0]].append(send)
+            dx, dy = DIRS[way]
+            owner = relative(owner[0] - dx * hops, owner[1] - dy * hops)
+            steps.append((now, next(count), "wait", (way, hops, chunk, owner, half)))
+            for message in allowed(way, chunk, owner, half):
+                put(message, now)
         for each in DIRS:
             begin(each, now)
-    return start, arrivals
+    return [(kind, message) for _, _, kind, message in sorted(steps)]
 
 
 def multi_indices():
@@ -112,7 +138,8 @@
     listing = multi_indices()
     lookup = {tuple(entry): number for number, entry in enumerate(listing)}
     targets = np.full((2 * KL, slots_all), -1, np.int32)
-    weights = np.zeros((2 * KL, slots_all), np.float32)
+    weights = np.zeros((2 * KL + 1, slots_all), np.float32)
+    weights[2 * KL, : len(listing)] = 1.0
     for number, entry in enumerate(listing):
         for variable in range(KL):
             for side, step in ((0, 1), (1, -1)):
@@ -123,12 +150,12 @@
                     weights[side * KL + variable, number] = math.sqrt(
                         max(entry[variable], other[variable])
                     )
-    return len(listing), targets, weights
+    return targets, weights
 
 
 def neighbour_tables(owner):
     slots_all = owner.shape[0]
-    number_all, targets, weights = chaos_tables(slots_all)
+    targets, weights = chaos_tables(slots_all)
     own = lax.dynamic_slice_in_dim(owner, lax.axis_index("chaos") * SLOTS_DEV, SLOTS_DEV, 0)
     numbers = jnp.arange(slots_all, dtype=jnp.int32)
     chosen = own[:, None, None] == numbers
@@ -136,8 +163,7 @@
     weight = jnp.sum(jnp.where(chosen, jnp.asarray(weights), 0.0), axis=-1)
     rows = (numbers // SLOTS_DEV) * BLOCK + (numbers % SLOTS_DEV) * PER_SLOT
     row = jnp.sum(jnp.where(target[:, :, None] == owner, rows, 0), axis=-1)
-    live = jnp.where(own < number_all, 1.0, 0.0)
-    return row, jnp.concatenate([weight, live[:, None]], axis=1)
+    return row, weight
 
 
 def kernel(
@@ -145,7 +171,8 @@
     weight_ref,
     disp_ref,
     load_ref,
-    moduli_ref,
+    mean_ref,
+    modes_ref,
     sol_ref,
     res_ref,
     gathered_0,
@@ -203,7 +230,8 @@
         return jnp.where(first_y, 0.0, pltpu.roll(f, 1, 1))
 
     barrier = pltpu.get_barrier_semaphore()
-    for dx, dy in DIRS.values():
+    peers = [*DIRS.values(), (2, 0), (0, 2), (0, -2)]
+    for dx, dy in peers:
         pl.semaphore_signal(
             barrier, inc=1, device_id=(chaos_at(dx, dy), slab), device_id_type=MESH
         )
@@ -234,7 +262,11 @@
     for v in range(KL + 1):
         mod[v] = zero
         for k in range(ROW):
-            mod[v, k : k + 1, :] = moduli_ref[v : v + 1, 128 * k : 128 * k + 128]
+            nodes = slice(128 * k, 128 * k + 128)
+            if v == 0:
+                mod[0, k, :] = mean_ref[nodes]
+            else:
+                mod[v, k : k + 1, :] = modes_ref[v - 1 : v, nodes]
 
     @pl.when(jnp.logical_not(has_low))
     def _():
@@ -255,7 +287,7 @@
 
         lax.fori_loop(0, ITERS * (SWEEPS + 1) * GROUPS, clear, 0)
 
-    neighbours = len(DIRS) + has_low.astype(jnp.int32) + has_high.astype(jnp.int32)
+    neighbours = len(peers) + has_low.astype(jnp.int32) + has_high.astype(jnp.int32)
     pl.semaphore_wait(barrier, neighbours)
 
     mod_copy = pltpu.make_async_remote_copy(
@@ -272,13 +304,17 @@
         mod_copy.start()
 
     blocks = (gathered_0, gathered_1)
-    start, arrivals = gather_plan()
-    ids = {arrival: number for number, (arrival, _) in enumerate(arrivals)}
-
-    def gather_copy(turn, way, part, owner, half):
-        dx, dy = DIRS[way]
-        number = ids[way, part, relative(owner[0] - dx, owner[1] - dy), half]
-        first, size = PIECES[part, half]
+    steps = gather_plan()
+    waits = [message for kind, message in steps if kind == "wait"]
+    ids = {message: number for number, message in enumerate(waits)}
+
+    def gather_copy(turn, kind, message):
+        way, hops, chunk, owner, half = message
+        dx, dy = (hops * d for d in DIRS[way])
+        if kind == "send":
+            message = (way, hops, chunk, relative(owner[0] - dx, owner[1] - dy), half)
+        number = ids[message]
+        first, size = piece_rows(chunk, half)
         base = chaos_at(*owner) * BLOCK + first
         piece = blocks[turn].at[pl.ds(pl.multiple_of(base, 8), size)]
         return pltpu.make_async_remote_copy(
@@ -400,8 +436,9 @@
     def iteration(turn):
         gathered = blocks[turn]
         gathered[pl.ds(pl.multiple_of(chaos * BLOCK, 8), BLOCK), :] = u_ref[...]
-        for message in start:
-            gather_copy(turn, *message).start()
+        began = steps.index(next(step for step in steps if step[0] == "wait"))
+        for kind, message in steps[:began]:
+            gather_copy(turn, kind, message).start()
 
         if turn == 0:
 
@@ -413,22 +450,11 @@
                 mod_x[v] = jnp.where(inside, down_x(mod[v]), 0.0)
                 mod_y[v] = down_y(mod[v])
 
-        for (way, part, owner, half), sends in arrivals:
-            dx, dy = DIRS[way]
-            first, size = PIECES[part, half]
-            base = chaos_at(*owner) * BLOCK + first
-            piece = blocks[turn].at[pl.ds(pl.multiple_of(base, 8), size)]
-            number = ids[way, part, owner, half]
-            pltpu.make_async_remote_copy(
-                src_ref=piece,
-                dst_ref=piece,
-                send_sem=ag_send.at[turn, number],
-                recv_sem=ag_recv.at[turn, number],
-                device_id=(chaos_at(dx, dy), slab),
-                device_id_type=MESH,
-            ).wait_recv()
-            for message in sends:
-                gather_copy(turn, *message).start()
+        for kind, message in steps[began:]:
+            if kind == "send":
+                gather_copy(turn, kind, message).start()
+            else:
+                gather_copy(turn, kind, message).wait_recv()
 
         def couple(g, _):
             i, _, _ = exchange(turn, 0, g)
@@ -522,11 +548,9 @@
         mod_copy.wait_send()
 
     for turn in range(ITERS):
-        for message in start:
-            gather_copy(turn, *message).wait_send()
-        for _, sends in arrivals:
-            for message in sends:
-                gather_copy(turn, *message).wait_send()
+        for kind, message in steps:
+            if kind == "send":
+                gather_copy(turn, kind, message).wait_send()
         for k in range(SWEEPS + 1):
             for g in range(GROUPS):
                 sent(turn, k, g)
@@ -534,9 +558,7 @@
 
 def per_device(displacement, load, mean_modulus, modes, owner):
     rows, weights = neighbour_tables(owner)
-    moduli = jnp.concatenate([mean_modulus[None], modes], axis=0)
-    _, arrivals = gather_plan()
-    messages = len(arrivals)
+    messages = sum(kind == "wait" for kind, _ in gather_plan())
     exchanges = ITERS * (SWEEPS + 1) * GROUPS
     field = pltpu.VMEM((BLOCK, 128), jnp.float32)
     moduli_field = pltpu.VMEM((KL + 1, 8, 128), jnp.float32)
@@ -547,7 +569,7 @@
     return pl.pallas_call(
         kernel,
         out_shape=(out, out),
-        in_specs=[smem, smem, vmem, vmem, vmem],
+        in_specs=[smem, smem, vmem, vmem, vmem, vmem],
         out_specs=(vmem, vmem),
         scratch_shapes=[
             pltpu.VMEM((PX * PY * BLOCK, 128), jnp.float32),
@@ -577,7 +599,7 @@
         ],
         compiler_params=pltpu.CompilerParams(collective_id=0, has_side_effects=True),
         name="galerkin",
-    )(rows, weights, displacement, load, moduli)
+    )(rows, weights, displacement, load, mean_modulus, modes)
 
 
 def solution(mesh):

time: 104 us -> 95.9 us (0.922)
  Pallas kernels: 95.9 us -> 89.2 us
    pallas_call x1, Pallas kernels: 95.9 us -> 89.2 us  [per_device(): pl.pallas_call(kernel, out_shape=(out, out), in_specs=[smem, smem, vmem,...]
    reduce_sum x1, other arithmetic: 0.12 us -> 1.49 us  [neighbour_tables(): weight = jnp.sum(jnp.where(chosen, jnp.asarray(weights), 0.0), axis=-1)]
    concatenate x2 -> x0, other arithmetic: 1.3 us -> none  [the longest x1 0.67 us: neighbour_tables(): return (row, jnp.concatenate([weight, live[:, None]], axis=1))]
    unnamed x12 -> x8, local copies, waits for them, and re-layouts: 2.69 us -> 2.91 us
where the time goes in v2:
time: 95.9 us; the launch traced here: 95.6 us
  Pallas kernels  89.2 us (93%)
  local copies, waits for them, and re-layouts  2.99 us (3%)
  other arithmetic  2.76 us (3%)
    pallas_call x1, Pallas kernels, per_device(): pl.pallas_call(kernel, out_shape=(out, out), in_specs=[smem, smem, vmem,...  89.2 us
    unnamed x8, local copies, waits for them, and re-layouts  2.91 us

profile of v2, /device:TPU:193, one launch (start us, length us, event | category | flops | bytes accessed | tf_op | source)
XLA Modules:
  0.0 95.6 jit_solution(8609697880750016666)
XLA Ops:
  0.6 0.0 copy-start.2
  0.6 0.0 copy-start.1
  0.7 0.7 copy-done.2
  1.3 0.1 dynamic_slice.3
  1.4 0.1 iota_compare_fusion
  1.5 1.5 %select_reduce_fusion.weight_ref = f32[9,21]{1,0:T(8,128)} fusion(f32[21,288]{1,0:T(8,128)} %constant.40.clone, pred[9,288]{1,0:T(8,128)(4,1)S(1)} %iota_compare_fusion), kind=kLoop, calls=%fused_computation | loop fusion | flops 108675 | bytes 27540 | tf_op jit(solution)/shard_map/reduce_sum | solution.py:163
  3.0 0.0 copy-done.1
  3.0 0.2 select_reduce_fusion.2
  3.2 0.9 select_reduce_fusion.1.rows_ref
  4.2 89.2 %galerkin.1 = (f32[9,3,768]{2,1,0:T(4,128)}, f32[9,3,768]{2,1,0:T(4,128)}) custom-call(s32[9,20]{1,0:T(8,128)} %select_reduce_fusion.1.rows_ref, f32[9,21]{1,0:T(8,128)} %select_reduce_fusion.weight_ref, f32[9,3,768]{2,1,0:T(4,128)} %disp_ref.1, f32[9,3,768]{2,1,0:T(4,128)} %load_ref.1, f32[768]{0:T(1024)} %mean_ref.1, f32[10,768]{1,0:T(8,128)} %modes_ref.1), custom_call_target="tpu_custom_call" | custom-call | tf_op jit(solution)/shard_map/galerkin/pallas_call | solution.py:569
  93.4 0.0 copy-start
  93.4 1.6 %copy.11 = f32[9,3,768]{2,1,0:T(4,128)} copy(f32[9,3,768]{2,1,0:T(4,128)} %get-tuple-element.4) | data formatting | bytes 165888
  95.0 0.0 copy-done
  95.0 0.6 copy.12
  (1 shorter events, 0.0 us)
Async XLA Ops:
  0.6 0.7 copy-start.2
  0.6 2.3 %copy-start.1 = (s32[20,288]{1,0:T(8,128)S(1)}, s32[20,288]{1,0:T(8,128)}, u32[]{:S(2)}) copy-start(s32[20,288]{1,0:T(8,128)} %constant.39.clone) | copy-start | bytes 69124
  93.4 1.6 %copy-start = (f32[9,3,768]{2,1,0:T(4,128)S(1)}, f32[9,3,768]{2,1,0:T(4,128)}, u32[]{:S(2)}) copy-start(f32[9,3,768]{2,1,0:T(4,128)} %get-tuple-element.5) | copy-start | bytes 248836

commit v3 on v2

--- a/solution.py
+++ b/solution.py
@@ -25,7 +25,7 @@
 DIRS = {"x+": (1, 0), "x-": (-1, 0), "y+": (0, 1), "y-": (0, -1)}
 CHUNKS = (("x", 0, 64, 32), ("y", 64, 104, 56))
 MODES = {("x", 0): "leap", ("y", 0): "leap", ("x", 1): "chain", ("y", 1): "chain"}
-LATENCY, HOP, RATE, AHEAD = 2.8, 0.8, 88.0, 1.2
+LATENCY, HOP, RATE, AHEAD = 3.4, 0.8, 80.0, 1.2
 
 
 def piece_rows(chunk, half):
@@ -137,44 +137,40 @@
 def chaos_tables(slots_all):
     listing = multi_indices()
     lookup = {tuple(entry): number for number, entry in enumerate(listing)}
-    targets = np.full((2 * KL, slots_all), -1, np.int32)
-    weights = np.zeros((2 * KL + 1, slots_all), np.float32)
-    weights[2 * KL, : len(listing)] = 1.0
+    packed = np.zeros((2 * KL + 1, slots_all), np.int32)
+    packed[2 * KL, : len(listing)] = 1
     for number, entry in enumerate(listing):
         for variable in range(KL):
             for side, step in ((0, 1), (1, -1)):
                 other = list(entry)
                 other[variable] += step
                 if tuple(other) in lookup:
-                    targets[side * KL + variable, number] = lookup[tuple(other)]
-                    weights[side * KL + variable, number] = math.sqrt(
-                        max(entry[variable], other[variable])
-                    )
-    return targets, weights
+                    square = max(entry[variable], other[variable])
+                    packed[side * KL + variable, number] = 4 * (lookup[tuple(other)] + 1) + square
+    return packed
 
 
 def neighbour_tables(owner):
     slots_all = owner.shape[0]
-    targets, weights = chaos_tables(slots_all)
     own = lax.dynamic_slice_in_dim(owner, lax.axis_index("chaos") * SLOTS_DEV, SLOTS_DEV, 0)
     numbers = jnp.arange(slots_all, dtype=jnp.int32)
     chosen = own[:, None, None] == numbers
-    target = jnp.sum(jnp.where(chosen, jnp.asarray(targets), 0), axis=-1)
-    weight = jnp.sum(jnp.where(chosen, jnp.asarray(weights), 0.0), axis=-1)
-    rows = (numbers // SLOTS_DEV) * BLOCK + (numbers % SLOTS_DEV) * PER_SLOT
-    row = jnp.sum(jnp.where(target[:, :, None] == owner, rows, 0), axis=-1)
-    return row, weight
+    packed = jnp.sum(jnp.where(chosen, jnp.asarray(chaos_tables(slots_all)), 0), axis=-1)
+    rows = 4 * ((numbers // SLOTS_DEV) * BLOCK + (numbers % SLOTS_DEV) * PER_SLOT)
+    found = (packed // 4)[:, :, None] == owner + 1
+    return jnp.sum(jnp.where(found, rows, 0), axis=-1) + packed % 4
 
 
 def kernel(
     rows_ref,
-    weight_ref,
     disp_ref,
     load_ref,
     mean_ref,
     modes_ref,
     sol_ref,
     res_ref,
+    row_of,
+    weight_of,
     gathered_0,
     gathered_1,
     u_ref,
@@ -206,6 +202,16 @@
     cx, cy = chaos // PY, chaos % PY
     has_low, has_high = slab > 0, slab < slabs - 1
 
+    def unpack(s, _):
+        for n in range(2 * KL):
+            entry = rows_ref[s, n]
+            square = lax.rem(entry, 4)
+            small = jnp.where(square == 1, 1.0, 0.0)
+            large = jnp.where(square == 2, math.sqrt(2.0), math.sqrt(3.0))
+            row_of[s, n] = lax.div(entry, 4)
+            weight_of[s, n] = jnp.where(square < 2, small, large)
+        return 0
+
     def chaos_at(dx, dy):
         return lax.rem(cx + dx + PX, PX) * PY + lax.rem(cy + dy + PY, PY)
 
@@ -248,14 +254,14 @@
         ref[BLOCK - 8 : BLOCK, :] = zero
 
     def take(s, _):
-        live = weight_ref[s, 2 * KL]
+        live = rows_ref[s, 2 * KL] == 1
         for c in range(3):
             for k in range(ROW):
                 at = pl.ds(s * PER_SLOT + c * ROW + k, 1)
                 piece = disp_ref[s, c : c + 1, 128 * k : 128 * k + 128]
-                u_ref[at, :] = jnp.where(live > 0.5, piece, 0.0)
+                u_ref[at, :] = jnp.where(live, piece, 0.0)
                 piece = load_ref[s, c : c + 1, 128 * k : 128 * k + 128]
-                f_ref[at, :] = jnp.where(live > 0.5, piece, 0.0)
+                f_ref[at, :] = jnp.where(live, piece, 0.0)
         return 0
 
     lax.fori_loop(0, SLOTS_DEV, take, 0)
@@ -441,6 +447,7 @@
             gather_copy(turn, kind, message).start()
 
         if turn == 0:
+            lax.fori_loop(0, SLOTS_DEV, unpack, 0)
 
             @pl.when(has_low)
             def _():
@@ -466,9 +473,8 @@
                 y = [mod_y[0] * e for e in u]
                 z = [mod_low[0] * e for e in u]
                 for v in range(1, KL + 1):
-                    up_row = rows_ref[s, v - 1]
-                    down_row = rows_ref[s, KL + v - 1]
-                    up_weight, down_weight = weight_ref[s, v - 1], weight_ref[s, KL + v - 1]
+                    up_row, up_weight = row_of[s, v - 1], weight_of[s, v - 1]
+                    down_row, down_weight = row_of[s, KL + v - 1], weight_of[s, KL + v - 1]
                     m, mx, my, mz = mod[v], mod_x[v], mod_y[v], mod_low[v]
                     for c in range(3):
                         e = up_weight * gathered[pl.ds(up_row + c * ROW, 8), :]
@@ -557,7 +563,7 @@
 
 
 def per_device(displacement, load, mean_modulus, modes, owner):
-    rows, weights = neighbour_tables(owner)
+    rows = neighbour_tables(owner)
     messages = sum(kind == "wait" for kind, _ in gather_plan())
     exchanges = ITERS * (SWEEPS + 1) * GROUPS
     field = pltpu.VMEM((BLOCK, 128), jnp.float32)
@@ -569,9 +575,11 @@
     return pl.pallas_call(
         kernel,
         out_shape=(out, out),
-        in_specs=[smem, smem, vmem, vmem, vmem, vmem],
+        in_specs=[smem, vmem, vmem, vmem, vmem],
         out_specs=(vmem, vmem),
         scratch_shapes=[
+            pltpu.SMEM((SLOTS_DEV, 2 * KL), jnp.int32),
+            pltpu.SMEM((SLOTS_DEV, 2 * KL), jnp.float32),
             pltpu.VMEM((PX * PY * BLOCK, 128), jnp.float32),
             pltpu.VMEM((PX * PY * BLOCK, 128), jnp.float32),
             field,
@@ -599,7 +607,7 @@
         ],
         compiler_params=pltpu.CompilerParams(collective_id=0, has_side_effects=True),
         name="galerkin",
-    )(rows, weights, displacement, load, mean_modulus, modes)
+    )(rows, displacement, load, mean_modulus, modes)
 
 
 def solution(mesh):

time: 95.9 us -> 94.4 us (0.984)
    reduce_sum x3 -> x2, other arithmetic: 2.67 us -> 1.35 us  [the longest x1 1.02 us: neighbour_tables(): jnp.sum(jnp.where(chosen, jnp.asarray(chaos_tables(slots_all)), 0), axis=-1)]
    unnamed x8 -> x6, local copies, waits for them, and re-layouts: 2.91 us -> 2.92 us
where the time goes in v3:
time: 94.4 us; the launch traced here: 94.1 us
  Pallas kernels  88.4 us (94%)
  local copies, waits for them, and re-layouts  2.99 us (3%)
  other arithmetic  2.07 us (2%)
    pallas_call x1, Pallas kernels, per_device(): pl.pallas_call(kernel, out_shape=(out, out), in_specs=[smem, vmem, vmem,...  88.4 us
    unnamed x6, local copies, waits for them, and re-layouts  2.92 us

profile of v3, /device:TPU:193, one launch (start us, length us, event | category | flops | bytes accessed | tf_op | source)
XLA Modules:
  0.0 94.1 jit_solution(12801013867101461797)
XLA Ops:
  0.6 0.0 copy-start.1
  0.6 0.7 copy-done.1
  1.3 0.1 dynamic_slice.3
  1.4 0.1 iota_compare_fusion
  1.5 1.0 %select_reduce_fusion.1 = s32[9,21]{1,0:T(8,128)S(1)} fusion(s32[21,288]{1,0:T(8,128)} %constant.62.clone, pred[9,288]{1,0:T(8,128)(4,1)S(1)} %iota_compare_fusion), kind=kLoop, calls=%fused_computation.1 | loop fusion | flops 108675 | bytes 27540 | tf_op jit(solution)/shard_map/reduce_sum | solution.py:158
  2.5 0.3 select_reduce_fusion
  2.8 0.6 fusion.rows_ref
  3.5 88.4 %galerkin.1 = (f32[9,3,768]{2,1,0:T(4,128)}, f32[9,3,768]{2,1,0:T(4,128)}) custom-call(s32[9,21]{1,0:T(8,128)} %fusion.rows_ref, f32[9,3,768]{2,1,0:T(4,128)} %disp_ref.1, f32[9,3,768]{2,1,0:T(4,128)} %load_ref.1, f32[768]{0:T(1024)} %mean_ref.1, f32[10,768]{1,0:T(8,128)} %modes_ref.1), custom_call_target="tpu_custom_call" | custom-call | tf_op jit(solution)/shard_map/galerkin/pallas_call | solution.py:575
  91.9 0.0 copy-start
  91.9 1.6 %copy.10 = f32[9,3,768]{2,1,0:T(4,128)} copy(f32[9,3,768]{2,1,0:T(4,128)} %get-tuple-element.6) | data formatting | bytes 165888
  93.5 0.0 copy-done
  93.5 0.6 copy.11
  (2 shorter events, 0.0 us)
Async XLA Ops:
  0.6 0.7 copy-start.1
  91.9 1.6 %copy-start = (f32[9,3,768]{2,1,0:T(4,128)S(1)}, f32[9,3,768]{2,1,0:T(4,128)}, u32[]{:S(2)}) copy-start(f32[9,3,768]{2,1,0:T(4,128)} %get-tuple-element.7) | copy-start | bytes 248836
